TPU v7x, 256 devices: a whole 4x4x8 slice. The times are simulated.
256 devices in a mesh: state: 256 (over y, z, x, core).
Axes of the slice: x: 4, y: 4, z: 8, core: 2. Of those that a mesh axis runs over, the one named last changes fastest.
Arguments:
- transitions: float32 [4096, 16, 4096], P('state'), may hold values from 0 to 1, as said below
- costs: float32 [4096, 16, 128], P('state'), may hold values from 0 to 4
- valid_counts: int32 [4096], P('state'), may hold values from 1 to 16
- start_values: float32 [4096, 128], P('state'), may hold values from -12 to 12
- ref_state: int32 [1], replicated, may hold values from 0 to 4095
Outputs:
- relative_values: float32 [4096, 128], P('state')
- lower_bounds: float32 [4, 128], replicated
- upper_bounds: float32 [4, 128], replicated
Inputs may be any that keep to these rules, and one draw needn't show every extreme that they name: Every entry is nonnegative and each row transitions[s, a, :] sums to one up to float32 rounding. Actions 0 to valid_counts[s] - 1 are allowed in state s.
All inputs are finite; a program needn't handle non-finite values.
Results may differ from a plain program's by a relative error of at most 0.00017.
Values sent between devices are 32-bit elements; how exact they have to be, the bound alone decides.
A program may use at most 64 MiB of HBM per device.

v0:
```python
import jax
import jax.numpy as jnp
from jax import lax
from jax.sharding import Mesh
from jax.sharding import PartitionSpec as P

ITERS = 4
STATE = ("state_0", "state_1", "state_2", "state_3")


big_value = 1e30


def over_axes(x, axes):
    for axis in axes:
        x = lax.pmax(x, axis)
    return x


def local(transitions, costs, valid_counts, start_values, ref_state):
    local_states = transitions.shape[0]
    actions = transitions.shape[1]
    scenarios = start_values.shape[1]
    flat_rows = transitions.reshape(local_states * actions, transitions.shape[2])
    allowed = jnp.arange(actions, dtype=jnp.int32)[None, :] < valid_counts[:, None]
    my_index = lax.axis_index(STATE)
    first_state = my_index * local_states
    owner_index = ref_state[0] // local_states
    offset = jnp.clip(ref_state[0] - first_state, 0, local_states - 1)
    is_owner = owner_index == my_index
    lower_list = []
    upper_list = []
    unshifted = start_values
    for iteration in range(ITERS):
        field_all = lax.all_gather(unshifted, STATE, axis=0, tiled=True)
        bellman_expected = jnp.dot(
            flat_rows,
            field_all,
            precision=lax.Precision.HIGHEST,
            preferred_element_type=jnp.float32,
        )
        q_values = costs + bellman_expected.reshape(local_states, actions, scenarios)
        q_values = jnp.where(allowed[:, :, None], q_values, jnp.float32(big_value))
        best_value = jnp.min(q_values, axis=1)
        increase = best_value - unshifted
        lower_list.append(jnp.min(increase, axis=0))
        upper_list.append(jnp.max(increase, axis=0))
        unshifted = best_value
    local_row = lax.dynamic_slice_in_dim(unshifted, offset, 1, 0)
    masked_row = jnp.where(is_owner, local_row, jnp.float32(-big_value))
    ref_row, upper_all, negated_all = (
        over_axes(masked_row, STATE),
        over_axes(jnp.stack(upper_list), STATE),
        over_axes(-jnp.stack(lower_list), STATE),
    )
    return (unshifted - ref_row, -negated_all, upper_all)


def solution(mesh):
    split = Mesh(mesh.devices.reshape(4, 8, 4, 2), ("state_0", "state_1", "state_2", "state_3"))
    return jax.shard_map(
        local,
        mesh=split,
        in_specs=(P(STATE, None, None), P(STATE, None, None), P(STATE), P(STATE, None), P()),
        out_specs=(P(STATE, None), P(), P()),
        check_vma=False,
    )
```

profile of v0, /device:TPU:1, one launch (start us, length us, event | category | flops | bytes accessed | tf_op | source)
XLA Modules:
  0.0 506.4 jit_solution(16758565774394789343)
XLA Ops:
  7.2 0.0 all-gather.5.cloned.1.call-start
  7.2 0.7 all-gather.5.cloned.1.call-update
  7.9 0.0 all-gather.7.cloned.1.call-start
  7.9 0.7 iota_compare_fusion
  8.7 111.4 %all-gather.5.cloned.1.call-done = f32[4096,128]{1,0:T(8,128)} async-done(((f32[16,128]{1,0:T(8,128)}), f32[4096,128]{1,0:T(8,128)}) %all-gather.5.cloned.1.call-update) | async-done | bytes 2097168 | tf_op jit(solution)/shard_map/all_gather | solution.py:35
  120.0 6.9 %fusion.8 = f32[16,128]{1,0:T(8,128)} fusion(f32[16,16,128]{2,1,0:T(8,128)} %param.6, f32[16,16,4096]{2,1,0:T(8,128)} %param.5, f32[4096,128]{1,0:T(8,128)} %all-gather.5.cloned.1.call-done, pred[16,16]{1,0:T(8,128)(4,1)S(1)} %iota_compare_fusion), kind=kOutput, calls=%fused_computation.7 | convolution fusion | flops 1610708992 | bytes 6430976 | tf_op jit(solution)/shard_map/dot_general | solution.py:36
  127.0 0.0 all-gather.7.cloned.1.call-update
  127.0 0.0 all-gather.9.cloned.1.call-start
  127.1 103.3 %all-gather.7.cloned.1.call-done = f32[4096,128]{1,0:T(8,128)} async-done(((f32[16,128]{1,0:T(8,128)}), f32[4096,128]{1,0:T(8,128)}) %all-gather.7.cloned.1.call-update) | async-done | bytes 2097168 | tf_op jit(solution)/shard_map/all_gather | solution.py:35
  230.3 6.3 %convolution_bitcast_fusion.2 = f32[256,128]{0,1:T(8,128)S(1)} fusion(f32[4096,128]{1,0:T(8,128)} %all-gather.7.cloned.1.call-done, f32[256,4096]{1,0:T(8,128)} %bitcast.44), kind=kOutput, calls=%fused_computation.6 | convolution fusion | flops 1610612736 | bytes 6422528 | tf_op jit(solution)/shard_map/dot_general | solution.py:36
  236.6 0.1 copy.8
  236.7 0.0 copy-done
  236.8 0.7 select_reduce_fusion.2
  237.5 0.0 all-gather.9.cloned.1.call-update
  237.5 0.2 all-gather.11.cloned.1.call-start
  237.7 103.1 %all-gather.9.cloned.1.call-done = f32[4096,128]{1,0:T(8,128)} async-done(((f32[16,128]{1,0:T(8,128)}), f32[4096,128]{1,0:T(8,128)}) %all-gather.9.cloned.1.call-update) | async-done | bytes 2097168 | tf_op jit(solution)/shard_map/all_gather | solution.py:35
  340.8 6.3 %convolution_bitcast_fusion.1 = f32[256,128]{0,1:T(8,128)S(1)} fusion(f32[4096,128]{1,0:T(8,128)} %all-gather.9.cloned.1.call-done, f32[256,4096]{1,0:T(8,128)} %bitcast.45), kind=kOutput, calls=%fused_computation.5 | convolution fusion | flops 1610612736 | bytes 6422528 | tf_op jit(solution)/shard_map/dot_general | solution.py:36
  347.1 0.1 copy.9
  347.2 0.7 select_reduce_fusion.1
  347.9 0.0 all-gather.11.cloned.1.call-update
  348.6 0.0 copy-start.1
  348.6 0.0 copy-start.4
  348.6 102.6 %all-gather.11.cloned.1.call-done = f32[4096,128]{1,0:T(8,128)} async-done(((f32[16,128]{1,0:T(8,128)}), f32[4096,128]{1,0:T(8,128)}) %all-gather.11.cloned.1.call-update) | async-done | bytes 2097168 | tf_op jit(solution)/shard_map/all_gather | solution.py:35
  451.2 6.3 %convolution_bitcast_fusion = f32[256,128]{0,1:T(8,128)S(1)} fusion(f32[4096,128]{1,0:T(8,128)} %all-gather.11.cloned.1.call-done, f32[256,4096]{1,0:T(8,128)} %bitcast.46), kind=kOutput, calls=%fused_computation.4 | convolution fusion | flops 1610612736 | bytes 6422528 | tf_op jit(solution)/shard_map/dot_general | solution.py:36
  457.5 0.1 copy.10
  457.6 0.1 select_reduce_fusion
  457.8 8.5 %all-reduce.2 = (f32[1,128]{1,0:T(1,128)S(1)}, f32[4,128]{1,0:T(4,128)S(1)}, f32[4,128]{1,0:T(4,128)S(1)}) all-reduce(f32[1,128]{1,0:T(1,128)S(1)} %broadcast_select_fusion, f32[4,128]{1,0:T(4,128)S(1)} %get-tuple-element.29, ...), channel_id=1, replica_groups=mesh['state_0'=4,'state_1'=8,'state_2'=4,'state_3'=2] {'state_0'}, use_global_device_ids=true, to_apply=%region_4.5 | all-reduce | flops 1152 | bytes 9216 | tf_op jit(solution)/shard_map/pmax | solution.py:16
  466.4 13.0 %all-reduce = (f32[1,128]{1,0:T(1,128)S(1)}, f32[4,128]{1,0:T(4,128)S(1)}, f32[4,128]{1,0:T(4,128)S(1)}) all-reduce(f32[1,128]{1,0:T(1,128)S(1)} %get-tuple-element.23, f32[4,128]{1,0:T(4,128)S(1)} %get-tuple-element.24, f32[4,128]{1,0:T(4,128)S(1)} %get-tuple-element.25), channel_id=1, replica_groups=mesh['state_0'=4,'state_1'=8,'state_2'=4,'state_3'=2] {'state_1'}, use_global_device_ids=true, to_apply=%region_5.6 | all-reduce | flops 1152 | bytes 9216 | tf_op jit(solution)/shard_map/pmax | solution.py:16
  479.4 8.5 %all-reduce.1 = (f32[1,128]{1,0:T(1,128)S(1)}, f32[4,128]{1,0:T(4,128)S(1)}, f32[4,128]{1,0:T(4,128)S(1)}) all-reduce(f32[1,128]{1,0:T(1,128)S(1)} %get-tuple-element.17, f32[4,128]{1,0:T(4,128)S(1)} %get-tuple-element.18, f32[4,128]{1,0:T(4,128)S(1)} %get-tuple-element.19), channel_id=1, replica_groups=mesh['state_0'=4,'state_1'=8,'state_2'=4,'state_3'=2] {'state_2'}, use_global_device_ids=true, to_apply=%region_6.7 | all-reduce | flops 1152 | bytes 9216 | tf_op jit(solution)/shard_map/pmax | solution.py:16
  487.9 10.8 %all-reduce.3 = (f32[128]{0:T(128)S(1)}, f32[4,128]{1,0:T(4,128)S(1)}, f32[4,128]{1,0:T(4,128)}) all-reduce(f32[128]{0:T(128)S(1)} %bitcast.55, f32[4,128]{1,0:T(4,128)S(1)} %get-tuple-element.21, f32[4,128]{1,0:T(4,128)S(1)} %get-tuple-element.22), channel_id=1, replica_groups=mesh['state_0'=4,'state_1'=8,'state_2'=4,'state_3'=2] {'state_3'}, use_global_device_ids=true, to_apply=%region_7.8 | all-reduce | flops 1152 | bytes 9216 | tf_op jit(solution)/shard_map/pmax | solution.py:16
  498.7 0.6 broadcast_subtract_fusion
  499.3 0.6 neg.7
  (10 shorter events, 0.1 us)
Async XLA Ops:
  7.2 112.9 %all-gather.5.cloned.1.call-start = ((), (), s32[]{:S(2)}) async-start(), calls=%async_computation | async-start | bytes 2105344 | tf_op jit(solution)/shard_map/all_gather | solution.py:35
  7.9 222.4 %all-gather.7.cloned.1.call-start = ((), (), s32[]{:S(2)}) async-start(), calls=%async_computation.1 | async-start | bytes 2105344 | tf_op jit(solution)/shard_map/all_gather | solution.py:35
  127.0 213.8 %all-gather.9.cloned.1.call-start = ((), (), s32[]{:S(2)}) async-start(), calls=%async_computation.2 | async-start | bytes 2105344 | tf_op jit(solution)/shard_map/all_gather | solution.py:35
  230.3 6.4 %copy-start = (f32[16,16,128]{2,1,0:T(8,128)S(1)}, f32[16,16,128]{2,1,0:T(8,128)}, u32[]{:S(2)}) copy-start(f32[16,16,128]{2,1,0:T(8,128)} %param.6) | copy-start | bytes 393220
  237.5 213.7 %all-gather.11.cloned.1.call-start = ((), (), s32[]{:S(2)}) async-start(), calls=%async_computation.3 | async-start | bytes 2105344 | tf_op jit(solution)/shard_map/all_gather | solution.py:35
  348.6 109.1 %copy-start.1 = (f32[16,128]{1,0:T(8,128)S(1)}, f32[16,128]{1,0:T(8,128)}, u32[]{:S(2)}) copy-start(f32[16,128]{1,0:T(8,128)} %fusion.8) | copy-start | bytes 24580
  348.6 109.1 %copy-start.2 = (f32[16,128]{1,0:T(8,128)S(1)}, f32[16,128]{1,0:T(8,128)}, u32[]{:S(2)}) copy-start(f32[16,128]{1,0:T(8,128)} %select_reduce_fusion.2) | copy-start | bytes 24580
  348.6 109.1 %copy-start.3 = (f32[16,128]{1,0:T(8,128)S(1)}, f32[16,128]{1,0:T(8,128)}, u32[]{:S(2)}) copy-start(f32[16,128]{1,0:T(8,128)} %select_reduce_fusion.1) | copy-start | bytes 24580
  348.6 109.1 %copy-start.4 = (f32[16,128]{1,0:T(8,128)S(1)}, f32[16,128]{1,0:T(8,128)}, u32[]{:S(2)}) copy-start(f32[16,128]{1,0:T(8,128)} %param.8) | copy-start | bytes 24580
Sparse Core Ops, SparseCore 0:
  11.7 108.2 all-gather.4
  127.1 103.1 all-gather.6
  237.6 103.1 all-gather.8
  348.0 103.1 all-gather.10
where the time goes:
time: 507 us; the launch traced here: 506 us
  waiting for transfers between devices  421 us (83%)
  blocking collectives  40.9 us (8%)
  matrix products  25.8 us (5%)
  between operations  14.6 us (3%)
    all_gather x4, waiting for transfers between devices, local(): field_all = lax.all_gather(unshifted, STATE, axis=0, tiled=True)  420 us
    pmax x4, blocking collectives, over_axes(): x = lax.pmax(x, axis)  40.9 us
    dot_general x4, matrix products, local(): jnp.dot(flat_rows, field_all, precision=lax.Precision.HIGHEST, preferred_...  25.8 us
  transfers between devices with their start and end apart: 4, of which 4 were waited for; matrix products, arithmetic and copies ran while one was open for 0% of the time, Pallas kernels for 0%

commit v1 on v0

v1 whole, which is shorter than its diff:
```python
import functools

import jax
import jax.numpy as jnp
from jax import lax
from jax.experimental import pallas as pl
from jax.experimental.pallas import tpu as pltpu
from jax.sharding import Mesh
from jax.sharding import PartitionSpec as P

ITERS = 4
AXES = ("y", "z", "x", "c")
BIG = 1e30


def kernel(
    dims,
    t_hbm, costs, counts, start, ref_state,
    out, lower, upper,
    stage, t_hi, t_lo, values, split, masked, red, red_z, red_a, red_b, red_c,
    load_sem, ssem_z, rsem_z, ssem_f, rsem_f, ssem_d, rsem_d, ssem_r, rsem_r,
):
    ny, nz, nx = dims
    n = ny
    states, scenarios = start.shape
    actions = costs.shape[0] // states
    rows, width = t_hi.shape
    y, z, x, c = (lax.axis_index(a) for a in AXES)

    def dev(yy, zz, xx, cc):
        return {"y": yy, "z": zz, "x": xx, "c": cc}

    def shift(k, second):
        along_x = c if not second else 1 - c
        return lax.rem(y + k * (1 - along_x), n), lax.rem(x + k * along_x, n)

    def both(ka, kb):
        ya, xa = shift(ka, False)
        yb, xb = shift(kb, True)
        return jnp.where(c == 0, ya, yb), jnp.where(c == 0, xb, xa)

    def remote(src, dst, ssem, rsem, to):
        return pltpu.make_async_remote_copy(
            src_ref=src, dst_ref=dst, send_sem=ssem, recv_sem=rsem,
            device_id=to, device_id_type=pl.DeviceIdType.MESH,
        )

    load = pltpu.make_async_copy(t_hbm, stage, load_sem)
    load.start()

    barrier = pltpu.get_barrier_semaphore()

    def greet(to):
        pl.semaphore_signal(barrier, inc=1, device_id=to, device_id_type=pl.DeviceIdType.MESH)

    def greet_z(d, _):
        greet(dev(y, lax.rem(z + d, nz), x, c))
        return 0

    lax.fori_loop(1, nz, greet_z, 0)

    def greet_plane(k, _):
        ya, xa = shift(k, False)
        greet(dev(ya, z, xa, c))
        yb, xb = shift(k, True)
        greet(dev(yb, z, xb, c))
        return 0

    lax.fori_loop(1, n, greet_plane, 0)
    greet(dev(y, z, x, 1 - c))

    values[0, y, z, x, c] = start[...]
    action = lax.broadcasted_iota(jnp.int32, (actions, scenarios), 0)
    for s in range(states):
        block = pl.ds(s * actions, actions)
        masked[block, :] = jnp.where(action < counts[s], costs[block, :], jnp.float32(BIG))

    pl.semaphore_wait(barrier, nz - 1 + 2 * (n - 1) + 1)

    def gather(t, p):
        own = values.at[t, y, z, x, c]

        def column(yy, xx):
            return values.at[t, yy, :, xx, c]

        def send_z(d, _):
            zz = lax.rem(z + d, nz)
            remote(own, own, ssem_z.at[d], rsem_z.at[p, z], dev(y, zz, x, c)).start()
            return 0

        lax.fori_loop(1, nz, send_z, 0)

        def wait_z(d, _):
            zz = lax.rem(z + d, nz)
            there = values.at[t, y, zz, x, c]
            remote(there, there, ssem_z.at[d], rsem_z.at[p, zz], dev(y, zz, x, c)).wait_recv()
            return 0

        lax.fori_loop(1, nz, wait_z, 0)

        def forward(k, yy, xx, second):
            def one(j, _):
                yt, xt = shift(j, second)
                slot = jnp.where(second, 1 + k, 0)
                remote(column(yy, xx), column(yy, xx), ssem_f.at[slot, j], rsem_f.at[p, yy, xx], dev(yt, z, xt, c)).start()
                return 0

            lax.fori_loop(1, n, one, 0)

        def across(yy, xx):
            remote(column(yy, xx), column(yy, xx), ssem_d.at[yy, xx], rsem_d.at[p, yy, xx], dev(y, z, x, 1 - c)).start()

        def arrived(yy, xx):
            remote(column(yy, xx), column(yy, xx), ssem_f.at[0, 0], rsem_f.at[p, yy, xx], dev(y, z, x, 1 - c)).wait_recv()

        forward(0, y, x, False)
        forward(0, y, x, True)
        across(y, x)

        def first(k, _):
            yy, xx = shift(k, False)
            arrived(yy, xx)
            forward(k, yy, xx, True)
            across(yy, xx)
            return 0

        lax.fori_loop(1, n, first, 0)

        def second(i, _):
            j = 1 + i // n
            yy, xx = both(i % n, j)
            arrived(yy, xx)
            across(yy, xx)
            return 0

        lax.fori_loop(0, (n - 1) * n, second, 0)

        def partner(i, _):
            yy, xx = i // n, i % n
            there = values.at[t, yy, :, xx, 1 - c]
            remote(there, there, ssem_d.at[yy, xx], rsem_d.at[p, yy, xx], dev(y, z, x, 1 - c)).wait_recv()
            remote(column(yy, xx), column(yy, xx), ssem_d.at[yy, xx], rsem_d.at[p, yy, xx], dev(y, z, x, 1 - c)).wait_send()
            return 0

        lax.fori_loop(0, n * n, partner, 0)

        def sent_z(d, _):
            remote(own, own, ssem_z.at[d], rsem_z.at[p, z], dev(y, z, x, 1 - c)).wait_send()
            return 0

        lax.fori_loop(1, nz, sent_z, 0)

        def sent_f(i, _):
            remote(column(y, x), column(y, x), ssem_f.at[i // (n - 1), 1 + i % (n - 1)], rsem_f.at[p, y, x], dev(y, z, x, 1 - c)).wait_send()
            return 0

        lax.fori_loop(0, (n + 1) * (n - 1), sent_f, 0)

    def split_rows():
        load.wait()

        def one(i, _):
            block = pl.ds(pl.multiple_of(i * 16, 16), 16)
            whole = stage[block, :]
            high = whole.astype(jnp.bfloat16)
            t_hi[block, :] = high
            t_lo[block, :] = (whole - high.astype(jnp.float32)).astype(jnp.bfloat16)
            return 0

        lax.fori_loop(0, rows // 16, one, 0)

    split_rows()
    per = nx * 2 * states

    def iterate(t, _):
        gather(t, lax.rem(t, 2))

        def halves(i, _):
            block = values[t, i // nz, i % nz].reshape(per, scenarios)
            high = block.astype(jnp.bfloat16)
            at = pl.ds(pl.multiple_of(i * per, per), per)
            split[at, :scenarios] = high
            split[at, scenarios:] = (block - high.astype(jnp.float32)).astype(jnp.bfloat16)
            return 0

        lax.fori_loop(0, ny * nz, halves, 0)
        right = split[...]
        total = jnp.dot(t_hi[...], right, preferred_element_type=jnp.float32)
        total += jnp.dot(t_lo[...], right, preferred_element_type=jnp.float32)
        q_values = masked[...] + (total[:, :scenarios] + total[:, scenarios:])
        best = jnp.min(q_values.reshape(states, actions, scenarios), axis=1)
        increase = best - values[t, y, z, x, c]
        red[pl.ds(t, 1), :] = jnp.max(increase, axis=0, keepdims=True)
        red[pl.ds(ITERS + t, 1), :] = jnp.max(-increase, axis=0, keepdims=True)

        @pl.when(t < ITERS - 1)
        def _():
            values[t + 1, y, z, x, c] = best

        @pl.when(t == ITERS - 1)
        def _():
            out[...] = best
        return 0

    lax.fori_loop(0, ITERS, iterate, 0)

    me = ((y * nz + z) * nx + x) * 2 + c
    row = me * states + lax.broadcasted_iota(jnp.int32, (states, scenarios), 0)
    ref_row = jnp.max(jnp.where(row == ref_state[0], out[...], jnp.float32(-BIG)), axis=0, keepdims=True)
    red[2 * ITERS:, :] = jnp.broadcast_to(ref_row, (8, scenarios))

    def exchange(buffer, count, index, to, sem):
        def go(d, _):
            remote(red, buffer.at[index(0)], ssem_r.at[sem + d], rsem_r.at[sem + index(0)], to(d)).start()
            return 0

        lax.fori_loop(1, count, go, 0)

        def done(d, _):
            remote(red, buffer.at[index(d)], ssem_r.at[sem + d], rsem_r.at[sem + index(d)], to(d)).wait()
            return 0

        lax.fori_loop(1, count, done, 0)
        best = red[...]
        for d in range(1, count):
            best = jnp.maximum(best, buffer[index(d)])
        red[...] = best

    exchange(red_z, nz, lambda d: lax.rem(z + d, nz), lambda d: dev(y, lax.rem(z + d, nz), x, c), 0)

    def place(second):
        def index(d):
            yy, xx = shift(d, second)
            along_x = c if not second else 1 - c
            return jnp.where(along_x == 1, xx, yy)

        def to(d):
            yy, xx = shift(d, second)
            return dev(yy, z, xx, c)

        return index, to

    exchange(red_a, n, *place(False), nz)
    exchange(red_b, n, *place(True), nz + n)
    exchange(red_c, 2, lambda d: lax.rem(c + d, 2), lambda d: dev(y, z, x, 1 - c), nz + 2 * n)

    upper[...] = red[:ITERS, :]
    lower[...] = -red[ITERS:2 * ITERS, :]
    out[...] = out[...] - red[2 * ITERS:2 * ITERS + 1, :]


def local(dims, transitions, costs, counts, start, ref_state):
    states, actions, width = transitions.shape
    scenarios = start.shape[1]
    rows = states * actions
    ny, nz, nx = dims
    n = ny
    block = (states, scenarios)
    dma = pltpu.SemaphoreType.DMA
    vmem = pl.BlockSpec(memory_space=pltpu.VMEM)
    smem = pl.BlockSpec(memory_space=pltpu.SMEM)
    return pl.pallas_call(
        functools.partial(kernel, dims),
        out_shape=(
            jax.ShapeDtypeStruct(block, jnp.float32),
            jax.ShapeDtypeStruct((ITERS, scenarios), jnp.float32),
            jax.ShapeDtypeStruct((ITERS, scenarios), jnp.float32),
        ),
        in_specs=[pl.BlockSpec(memory_space=pl.ANY), vmem, smem, vmem, smem],
        out_specs=(vmem, vmem, vmem),
        scratch_shapes=[
            pltpu.VMEM((rows, width), jnp.float32),
            pltpu.VMEM((rows, width), jnp.bfloat16),
            pltpu.VMEM((rows, width), jnp.bfloat16),
            pltpu.VMEM((ITERS, ny, nz, nx, 2) + block, jnp.float32),
            pltpu.VMEM((width, 2 * scenarios), jnp.bfloat16),
            pltpu.VMEM((rows, scenarios), jnp.float32),
            pltpu.VMEM(block, jnp.float32),
            pltpu.VMEM((nz,) + block, jnp.float32),
            pltpu.VMEM((n,) + block, jnp.float32),
            pltpu.VMEM((n,) + block, jnp.float32),
            pltpu.VMEM((2,) + block, jnp.float32),
            dma,
            dma((nz,)),
            dma((2, nz)),
            dma((n + 1, n)),
            dma((2, n, n)),
            dma((n, n)),
            dma((2, n, n)),
            dma((nz + 2 * n + 2,)),
            dma((nz + 2 * n + 2,)),
        ],
        compiler_params=pltpu.CompilerParams(collective_id=0, has_side_effects=True),
    )(transitions.reshape(rows, width), costs.reshape(rows, scenarios), counts, start, ref_state)


def solution(mesh):
    dims = (4, 8, 4)
    split = Mesh(mesh.devices.reshape(dims + (2,)), AXES)
    return jax.shard_map(
        functools.partial(local, dims),
        mesh=split,
        in_specs=(P(AXES, None, None), P(AXES, None, None), P(AXES), P(AXES, None), P()),
        out_specs=(P(AXES, None), P(), P()),
        check_vma=False,
    )
```

time: 507 us -> 119 us (0.23)
  waiting for transfers between devices: 421 us -> 0 us
  Pallas kernels: 0 us -> 113 us
  blocking collectives: 40.9 us -> 0 us
  matrix products: 25.8 us -> 0 us
  between operations: 14.6 us -> 1.29 us
    all_gather x4 -> x0, waiting for transfers between devices: 420 us -> none  [local(): field_all = lax.all_gather(unshifted, STATE, axis=0, tiled=True)]
    pallas_call x0 -> x1, Pallas kernels: none -> 113 us  [local(): pl.pallas_call(functools.partial(kernel, dims), out_shape=(jax.ShapeDtype...]
    pmax x4 -> x0, blocking collectives: 40.9 us -> none  [over_axes(): x = lax.pmax(x, axis)]
    dot_general x4 -> x0, matrix products: 25.8 us -> none  [local(): jnp.dot(flat_rows, field_all, precision=lax.Precision.HIGHEST, preferred_...]
  transfers between devices with their start and end apart: 4 -> 0, of which waited for: 4 -> 0; matrix products, arithmetic and copies ran while one was open for 0% -> 0% of each run, Pallas kernels for 0% -> 0%
where the time goes in v1:
time: 119 us; the launch traced here: 118 us
  Pallas kernels  113 us (95%)
  local copies, waits for them, and re-layouts  3.77 us (3%)
  between operations  1.29 us (1%)
    pallas_call x1, Pallas kernels, local(): pl.pallas_call(functools.partial(kernel, dims), out_shape=(jax.ShapeDtype...  113 us
    unnamed x3, local copies, waits for them, and re-layouts  3.77 us

profile of v1, /device:TPU:1, one launch (start us, length us, event | category | flops | bytes accessed | tf_op | source)
XLA Modules:
  0.0 118.4 jit_solution(13229481145688190926)
XLA Ops:
  1.3 113.3 %shard_map.76 = (f32[16,128]{1,0:T(8,128)}, f32[4,128]{1,0:T(4,128)}, f32[4,128]{1,0:T(4,128)}) custom-call(f32[256,4096]{1,0:T(8,128)} %bitcast.2, f32[256,128]{1,0:T(8,128)} %bitcast.3, s32[16]{0:T(128)} %counts.1, f32[16,128]{1,0:T(8,128)} %start.1, s32[1]{0:T(128)S(6)} %copy.11.ref_state), custom_call_target="tpu_custom_call" | custom-call | tf_op jit(solution)/shard_map/pallas_call | solution.py:262
  114.6 1.3 %copy.12 = f32[16,128]{1,0:T(8,128)} copy(f32[16,128]{1,0:T(8,128)} %get-tuple-element.6) | data formatting | bytes 16384
  115.9 1.2 %copy.13 = f32[4,128]{1,0:T(4,128)} copy(f32[4,128]{1,0:T(4,128)} %get-tuple-element.7) | data formatting | bytes 4096
  117.1 1.2 %copy.14 = f32[4,128]{1,0:T(4,128)} copy(f32[4,128]{1,0:T(4,128)} %get-tuple-element.8) | data formatting | bytes 4096
